TPU v7x, 32 devices: a whole 2x2x4 slice. The times are simulated.
32 devices in a mesh: seq: 16 (over z, x, core), tp: 2 (over y).
Axes of the slice: x: 2, y: 2, z: 4, core: 2. Of those that a mesh axis runs over, the one named last changes fastest.
Arguments:
- hidden_in: bfloat16 [2048, 4096], P('seq', 'tp'), may hold values from -64 to 64
- span_order: int32 [16], replicated, may hold values from 0 to 15, each once
- norm_gain: bfloat16 [4096], P('tp'), may hold values from 0.099609375 to 1.8984375
- w_query: bfloat16 [4096, 4096], P('seq', 'tp'), may hold values from -0.09375 to 0.09375
- bias_query: bfloat16 [4096], P('tp'), may hold values from -14 to 14
- key_value_weight: bfloat16 [4096, 2, 1024], P('seq', None, 'tp'), may hold values from -0.09375 to 0.09375
- bias_kv: bfloat16 [2, 1024], P(None, 'tp'), may hold values from -14 to 14
- w_out: bfloat16 [4096, 4096], P('tp', 'seq'), may hold values from -0.09375 to 0.09375
- post_gain: bfloat16 [4096], P('tp'), may hold values from 0.099609375 to 1.8984375
Outputs:
- attn_out: bfloat16 [2048, 4096], P('seq', 'tp')
- normed: bfloat16 [2048, 4096], P('seq', 'tp')
Inputs may be any that keep to these rules, and one draw needn't show every extreme that they name: Each span number appears once; row r of hidden_in belongs to span span_order[r // 128].
All inputs are finite; a program needn't handle non-finite values.
Results may differ from a plain program's by a relative error of at most 0.014.
Values may be sent and summed in bfloat16 or wider, within the bound.
A program may use at most 128 MiB of HBM per device.

v0:
```python
import math
import jax
import jax.numpy as jnp
from jax import lax
from jax.sharding import PartitionSpec as P

MODEL_WIDTH = 4096
HEAD_SIZE = 128
GROUP = 4
eps = 1e-06
rope_base = 1000000.0


def apply_rotary(field, token_positions):
    half = field.shape[-1] // 2
    inverse = jnp.exp(-math.log(rope_base) * jnp.arange(half, dtype=jnp.float32) / half)
    angles = token_positions.astype(jnp.float32)[:, None] * inverse[None, :]
    cosine = jnp.cos(angles)[:, None, :]
    sine = jnp.sin(angles)[:, None, :]
    first = field[..., :half]
    second = field[..., half:]
    return jnp.concatenate(
        [first * cosine - second * sine, second * cosine + first * sine], axis=-1
    )


def span_lookup(order, devices):
    table_ids = jnp.arange(order.shape[0], dtype=jnp.int32)
    return jnp.sum(jnp.where(devices[:, None] == table_ids[None, :], order[None, :], 0), axis=1)


def per_device(
    hidden_in,
    span_order,
    norm_gain,
    w_query,
    bias_query,
    key_value_weight,
    bias_kv,
    w_out,
    post_gain,
):
    tok_rows = hidden_in.shape[0]
    seq_index = lax.axis_index("seq")
    own_span = span_lookup(span_order, jnp.full((1,), seq_index, jnp.int32))[0]
    token_positions = own_span * tok_rows + jnp.arange(tok_rows, dtype=jnp.int32)
    local = hidden_in.astype(jnp.float32)
    raw_rows, gains = (
        lax.all_gather(hidden_in, "tp", axis=1, tiled=True),
        lax.all_gather(norm_gain[None, :], "tp", axis=1, tiled=True),
    )
    full_rows = raw_rows.astype(jnp.float32)
    meansq = jnp.mean(full_rows * full_rows, axis=1, keepdims=True)
    normed_in = (full_rows * lax.rsqrt(meansq + eps) * gains.astype(jnp.float32)).astype(
        jnp.bfloat16
    )
    columns = normed_in
    query_proj = jnp.dot(
        columns,
        lax.all_gather(w_query, "seq", axis=0, tiled=True),
        preferred_element_type=jnp.float32,
    )
    columns = normed_in
    pair_proj = jnp.einsum(
        "tr,rkc->tkc",
        columns,
        lax.all_gather(key_value_weight, "seq", axis=0, tiled=True),
        preferred_element_type=jnp.float32,
    )
    query_heads = w_query.shape[1] // HEAD_SIZE
    kv_heads = key_value_weight.shape[2] // HEAD_SIZE
    query_proj = query_proj + bias_query.astype(jnp.float32)[None, :]
    queries = apply_rotary(
        query_proj.reshape(tok_rows, query_heads, HEAD_SIZE), token_positions
    ).astype(jnp.bfloat16)
    pair_proj = pair_proj + bias_kv.astype(jnp.float32)[None, :, :]
    rotated_keys = apply_rotary(
        pair_proj[:, 0, :].reshape(tok_rows, kv_heads, HEAD_SIZE), token_positions
    )
    rotated_keys = rotated_keys.astype(jnp.bfloat16).reshape(tok_rows, kv_heads * HEAD_SIZE)
    value_rows = pair_proj[:, 1, :].astype(jnp.bfloat16)
    grouped = (
        queries.reshape(tok_rows, kv_heads, GROUP, HEAD_SIZE)
        .transpose(1, 2, 0, 3)
        .reshape(kv_heads, GROUP * tok_rows, HEAD_SIZE)
    )
    query_pos = jnp.tile(token_positions, GROUP)
    last_query = jnp.max(token_positions)
    scale = 1.0 / math.sqrt(HEAD_SIZE)
    start_state = (
        jnp.full((kv_heads, GROUP * tok_rows), -1e30, jnp.float32),
        jnp.zeros((kv_heads, GROUP * tok_rows), jnp.float32),
        jnp.zeros((kv_heads, GROUP * tok_rows, HEAD_SIZE), jnp.float32),
    )
    key_piece = lax.all_gather(rotated_keys, "seq", axis=0, tiled=True)
    value_piece = lax.all_gather(value_rows, "seq", axis=0, tiled=True)
    count = key_piece.shape[0]
    block = math.gcd(count, 1536)

    def visit(step, state):
        first = step * block
        key_block = lax.dynamic_slice_in_dim(key_piece, first, block, 0).reshape(
            block, kv_heads, HEAD_SIZE
        )
        value_block = lax.dynamic_slice_in_dim(value_piece, first, block, 0).reshape(
            block, kv_heads, HEAD_SIZE
        )
        row_ids = first + jnp.arange(block, dtype=jnp.int32)
        key_pos = span_lookup(span_order, row_ids // tok_rows) * tok_rows + row_ids % tok_rows

        def update(current):
            maxima, totals, sums = current
            scores = (
                jnp.einsum("kqd,nkd->kqn", grouped, key_block, preferred_element_type=jnp.float32)
                * scale
            )
            allowed = (key_pos[None, :] <= query_pos[:, None])[None, :, :]
            scores = jnp.where(allowed, scores, -1e30)
            fresh = jnp.maximum(maxima, jnp.max(scores, axis=2))
            weights = jnp.where(allowed, jnp.exp(scores - fresh[:, :, None]), 0.0)
            factor = jnp.exp(maxima - fresh)
            totals = totals * factor + jnp.sum(weights, axis=2)
            sums = sums * factor[:, :, None] + jnp.einsum(
                "kqn,nkd->kqd",
                weights.astype(jnp.bfloat16),
                value_block,
                preferred_element_type=jnp.float32,
            )
            return (fresh, totals, sums)

        return lax.cond(jnp.min(key_pos) <= last_query, update, lambda current: current, state)

    maxima, totals, sums = lax.fori_loop(0, count // block, visit, start_state)
    attended = (sums / totals[:, :, None]).astype(jnp.bfloat16)
    attended = (
        attended.reshape(kv_heads, GROUP, tok_rows, HEAD_SIZE)
        .transpose(2, 0, 1, 3)
        .reshape(tok_rows, query_heads * HEAD_SIZE)
    )
    partial_out = jnp.dot(
        attended,
        lax.all_gather(w_out, "seq", axis=1, tiled=True),
        preferred_element_type=jnp.float32,
    )
    mixed = lax.psum_scatter(
        partial_out.astype(jnp.bfloat16), "tp", scatter_dimension=1, tiled=True
    ).astype(jnp.float32)
    attn_out = mixed.astype(jnp.bfloat16)
    stream = local + mixed
    post_sq = lax.psum(jnp.sum(stream * stream, axis=1), "tp")
    normed = (
        stream
        * lax.rsqrt(post_sq / MODEL_WIDTH + eps)[:, None]
        * post_gain.astype(jnp.float32)[None, :]
    ).astype(jnp.bfloat16)
    return (attn_out, normed)


def solution(mesh):
    placed = (
        P("seq", "tp"),
        P(),
        P("tp"),
        P("seq", "tp"),
        P("tp"),
        P("seq", None, "tp"),
        P(None, "tp"),
        P("tp", "seq"),
        P("tp"),
    )
    return jax.shard_map(
        per_device,
        mesh=mesh,
        in_specs=placed,
        out_specs=(P("seq", "tp"), P("seq", "tp")),
        check_vma=False,
    )
```

profile of v0, /device:TPU:0, one launch (start us, length us, event | category | flops | bytes accessed | tf_op | source)
XLA Modules:
  0.0 499.7 jit_solution(17849845767442077635)
XLA Ops:
  7.2 0.7 all-gather.9.cloned.1.call-update
  7.9 1.9 copy.44
  9.9 5.5 %all-gather = bf16[4096]{0:T(1024)(128)(2,1)S(1)} all-gather(bf16[2048]{0:T(1024)(128)(2,1)} %param.15), channel_id=2, replica_groups=mesh['seq'=16,'tp'=2] {'tp'}, dimensions={0}, use_global_device_ids=true | all-gather | bytes 12288 | tf_op jit(solution)/shard_map/all_gather | solution.py:50
  15.4 0.7 convert_element_type.69
  16.1 17.4 %all-gather.9.cloned.1.call-done = bf16[128,4096]{1,0:T(8,128)(2,1)} async-done(((bf16[128,2048]{1,0:T(8,128)(2,1)}), bf16[128,4096]{1,0:T(8,128)(2,1)}) %all-gather.9.cloned.1.call-update) | async-done | bytes 1048592 | tf_op jit(solution)/shard_map/all_gather | solution.py:49
  33.6 1.5 fusion.18
  35.1 75.6 %all-gather.11.cloned.1.call-done = bf16[4096,2,512]{2,0,1:T(8,128)(2,1)} async-done(((bf16[256,2,512]{2,0,1:T(8,128)(2,1)}), bf16[4096,2,512]{2,0,1:T(8,128)(2,1)}) %all-gather.11.cloned.1.call-update) | async-done | bytes 8388624 | tf_op jit(solution)/shard_map/all_gather | solution.py:67
  110.7 5.0 %convolution_add_fusion.1 = f32[128,2,512]{2,0,1:T(8,128)S(1)} fusion(bf16[4096,2,512]{2,0,1:T(8,128)(2,1)} %all-gather.11.cloned.1.call-done, bf16[128,4096]{1,0:T(8,128)(2,1)} %all-gather.9.cloned.1.call-done, f32[4096]{0:T(1024)S(1)} %mul.210, f32[128]{0:T(128)S(1)} %add_rsqrt_fusion.1, f32[2,512]{1,0:T(2,128)S(1)} %convert_element_type.69), kind=kOutput, calls=%fused_computation.39 | convolution fusion | flops 1075970048 | bytes 9982464 | tf_op jit(solution)/shard_map/tr,rkc->tkc/dot_general | solution.py:64
  115.7 0.7 slice.40
  116.4 0.5 all-gather.15.cloned.1.call-update
  117.0 0.6 fusion.25
  118.4 0.3 multiply_cosine_fusion
  118.8 0.3 subtract_convert_fusion.1
  119.3 0.8 copy.45
  120.1 0.5 all-gather.17.cloned.1.call-update
  120.7 0.2 reduce-scatter.2.cloned.1.call-start
  120.9 0.6 iota_add_fusion.1
  121.5 35.1 %all-gather.19.cloned.1.call-done = bf16[2048,1,512]{2,0,1:T(8,128)(2,1)} async-done(((bf16[128,1,512]{2,0,1:T(8,128)(2,1)}), bf16[2048,1,512]{2,0,1:T(8,128)(2,1)}) %all-gather.19.cloned.1.call-update) | async-done | bytes 2097168 | tf_op jit(solution)/shard_map/all_gather | solution.py:96
  156.6 2.9 copy.48
  159.5 124.3 %all-gather.15.cloned.1.call-done = bf16[4096,2048]{1,0:T(8,128)(2,1)} async-done(((bf16[256,2048]{1,0:T(8,128)(2,1)}), bf16[4096,2048]{1,0:T(8,128)(2,1)}) %all-gather.15.cloned.1.call-update) | async-done | bytes 16777232 | tf_op jit(solution)/shard_map/all_gather | solution.py:60
  283.8 8.2 %fusion.21 = f32[16,8,16,128]{3,1,2,0:T(8,128)S(1)} fusion(bf16[4096,2048]{1,0:T(8,128)(2,1)} %all-gather.15.cloned.1.call-done, f32[2048]{0:T(1024)S(1)} %convert_element_type.72, bf16[128,4096]{1,0:T(8,128)(2,1)S(1)} %copy-done, f32[4096]{0:T(1024)S(1)} %mul.210, f32[128]{0:T(128)S(1)} %add_rsqrt_fusion.1), kind=kOutput, calls=%fused_computation.38 | convolution fusion | flops 2149842944 | bytes 18899456 | tf_op jit(solution)/shard_map/dot_general | solution.py:58
  292.2 0.5 subtract_convert_fusion
  293.0 0.3 pad_maximum_fusion
  293.3 32.3 %all-gather.13.cloned.1.call-done = bf16[2048,512]{0,1:T(8,128)(2,1)} async-done(((bf16[128,512]{0,1:T(8,128)(2,1)}), bf16[2048,512]{0,1:T(8,128)(2,1)}) %all-gather.13.cloned.1.call-update) | async-done | bytes 2097168 | tf_op jit(solution)/shard_map/all_gather | solution.py:95
  325.6 1.1 broadcast_in_dim.105
  326.7 33.3 %while.20 = (s32[]{:T(128)}, f32[4,512]{1,0:T(4,128)S(1)}, f32[4,512]{1,0:T(4,128)S(1)}, f32[4,512,128]{2,1,0:T(8,128)}, s32[16]{0:T(128)S(1)}, /*index=5*/s32[]...) while((s32[]{:T(128)}, f32[4,512]{1,0:T(4,128)S(1)}, ...), condition=%wide.region_10.11_spmd.clone, body=%wide.region_3.10_spmd.clone.sunk | while | flops 551332864 | bytes 27935672 | solution.py:133
  326.8 0.6 fusion.38
  328.7 6.3 %conditional.3 = ((f32[4,512]{1,0:T(4,128)S(1)}, f32[4,512]{1,0:T(4,128)S(1)}, f32[4,512,128]{2,1,0:T(8,128)})) conditional(s32[]{:T(128)} %convert_element_type.117, (f32[4,512]{1,0:T(4,128)S(1)}, f32[4,512]{1,0:T(4,128)S(1)}, f32[4,512,128]{2,1,0:T(8,128)}) %tuple.77, (s32[512]{0:T(512)S(1)}, s32[128]{0:T(128)S(1)}, s32[]{:T(128)}, ...), branch_computations={%region_6.6_spmd, %region_7.9_spmd} | conditional | flops 551292928 | bytes 27925118 | solution.py:131
  328.7 1.1 constant_dynamic-slice_fusion
  329.9 0.2 broadcast_compare_fusion
  330.1 1.0 fusion.2
  331.2 1.0 fusion.4
  332.2 1.8 fusion.8
  334.0 1.0 copy-done.3
  335.1 0.6 fusion.38
  337.0 6.3 %conditional.3 = ((f32[4,512]{1,0:T(4,128)S(1)}, f32[4,512]{1,0:T(4,128)S(1)}, f32[4,512,128]{2,1,0:T(8,128)})) conditional(s32[]{:T(128)} %convert_element_type.117, (f32[4,512]{1,0:T(4,128)S(1)}, f32[4,512]{1,0:T(4,128)S(1)}, f32[4,512,128]{2,1,0:T(8,128)}) %tuple.77, (s32[512]{0:T(512)S(1)}, s32[128]{0:T(128)S(1)}, s32[]{:T(128)}, ...), branch_computations={%region_6.6_spmd, %region_7.9_spmd} | conditional | flops 551292928 | bytes 27925118 | solution.py:131
  337.0 1.2 constant_dynamic-slice_fusion
  338.2 0.2 broadcast_compare_fusion
  338.5 1.0 fusion.2
  339.5 1.0 fusion.4
  340.6 1.8 fusion.8
  342.4 1.0 copy-done.3
  343.5 0.6 fusion.38
  345.4 6.3 %conditional.3 = ((f32[4,512]{1,0:T(4,128)S(1)}, f32[4,512]{1,0:T(4,128)S(1)}, f32[4,512,128]{2,1,0:T(8,128)})) conditional(s32[]{:T(128)} %convert_element_type.117, (f32[4,512]{1,0:T(4,128)S(1)}, f32[4,512]{1,0:T(4,128)S(1)}, f32[4,512,128]{2,1,0:T(8,128)}) %tuple.77, (s32[512]{0:T(512)S(1)}, s32[128]{0:T(128)S(1)}, s32[]{:T(128)}, ...), branch_computations={%region_6.6_spmd, %region_7.9_spmd} | conditional | flops 551292928 | bytes 27925118 | solution.py:131
  345.4 1.1 constant_dynamic-slice_fusion
  346.8 1.0 fusion.2
  347.8 1.0 fusion.4
  348.9 1.8 fusion.8
  350.7 1.0 copy-done.3
  351.8 0.6 fusion.38
  353.7 6.3 %conditional.3 = ((f32[4,512]{1,0:T(4,128)S(1)}, f32[4,512]{1,0:T(4,128)S(1)}, f32[4,512,128]{2,1,0:T(8,128)})) conditional(s32[]{:T(128)} %convert_element_type.117, (f32[4,512]{1,0:T(4,128)S(1)}, f32[4,512]{1,0:T(4,128)S(1)}, f32[4,512,128]{2,1,0:T(8,128)}) %tuple.77, (s32[512]{0:T(512)S(1)}, s32[128]{0:T(128)S(1)}, s32[]{:T(128)}, ...), branch_computations={%region_6.6_spmd, %region_7.9_spmd} | conditional | flops 551292928 | bytes 27925118 | solution.py:131
  353.7 1.1 constant_dynamic-slice_fusion
  355.1 1.0 fusion.2
  356.1 1.0 fusion.4
  357.2 1.8 fusion.8
  359.0 1.0 copy-done.3
  360.0 1.6 divide_convert_fusion
  361.6 0.3 copy.49
  361.8 94.8 %all-gather.17.cloned.1.call-done = bf16[2048,4096]{1,0:T(8,128)(2,1)} async-done(((bf16[2048,256]{1,0:T(8,128)(2,1)}), bf16[2048,4096]{1,0:T(8,128)(2,1)}) %all-gather.17.cloned.1.call-update) | async-done | bytes 16777232 | tf_op jit(solution)/shard_map/all_gather | solution.py:142
  456.6 9.2 %convolution_convert_fusion = bf16[128,4096]{1,0:T(8,128)(2,1)} fusion(bf16[128,2048]{0,1:T(8,128)(2,1)S(1)} %bitcast.47, bf16[2048,4096]{1,0:T(8,128)(2,1)} %all-gather.17.cloned.1.call-done), kind=kOutput, calls=%fused_computation.31 | convolution fusion | flops 2148007936 | bytes 18350080 | tf_op jit(solution)/shard_map/dot_general | solution.py:140
  465.9 18.7 %reduce-scatter.2.cloned.1.call-done = bf16[128,2048]{1,0:T(8,128)(2,1)} async-done(((bf16[128,4096]{1,0:T(8,128)(2,1)}), bf16[128,2048]{1,0:T(8,128)(2,1)}) %reduce-scatter.2.cloned.1.call-update) | async-done | bytes 524304 | tf_op jit(solution)/shard_map/reduce_scatter | solution.py:145
  484.6 1.3 multiply_reduce_fusion
  485.9 4.9 psum.7
  490.8 2.0 multiply_convert_fusion
  (73 shorter events, 2.1 us)
Async XLA Ops:
  7.2 26.4 %all-gather.9.cloned.1.call-start = ((), (), s32[]{:S(2)}) async-start(), calls=%async_computation.1 | async-start | bytes 1572864 | tf_op jit(solution)/shard_map/all_gather | solution.py:49
  7.9 102.8 %all-gather.11.cloned.1.call-start = ((), (), s32[]{:S(2)}) async-start(), calls=%async_computation.2 | async-start | bytes 8912896 | tf_op jit(solution)/shard_map/all_gather | solution.py:67
  9.9 146.8 %all-gather.19.cloned.1.call-start = ((), (), s32[]{:S(2)}) async-start(), calls=%async_computation.7 | async-start | bytes 2228224 | tf_op jit(solution)/shard_map/all_gather | solution.py:96
  35.1 81.9 %copy-start.4 = (s32[16]{0:T(128)S(1)}, s32[16]{0:T(128)}, u32[]{:S(2)}) copy-start(s32[16]{0:T(128)} %param.14) | copy-start | bytes 196
  115.7 5.2 %copy-start.5 = (bf16[2048]{0:T(1024)(128)(2,1)S(1)}, bf16[2048]{0:T(1024)(128)(2,1)}, u32[]{:S(2)}) copy-start(bf16[2048]{0:T(1024)(128)(2,1)} %param.17) | copy-start | bytes 12292
  116.4 167.4 %all-gather.15.cloned.1.call-start = ((), (), s32[]{:S(2)}) async-start(), calls=%async_computation.4 | async-start | bytes 17825792 | tf_op jit(solution)/shard_map/all_gather | solution.py:60
  117.0 166.8 %copy-start = (bf16[128,4096]{1,0:T(8,128)(2,1)S(1)}, bf16[128,4096]{1,0:T(8,128)(2,1)}, u32[]{:S(2)}) copy-start(bf16[128,4096]{1,0:T(8,128)(2,1)} %all-gather.9.cloned.1.call-done) | copy-start | bytes 3145732
  117.0 208.7 %all-gather.13.cloned.1.call-start = ((), (), s32[]{:S(2)}) async-start(), calls=%async_computation.3 | async-start | bytes 2228224 | tf_op jit(solution)/shard_map/all_gather | solution.py:95
  120.1 336.6 %all-gather.17.cloned.1.call-start = ((), (), s32[]{:S(2)}) async-start(), calls=%async_computation.5 | async-start | bytes 17825792 | tf_op jit(solution)/shard_map/all_gather | solution.py:142
  120.7 363.9 %reduce-scatter.2.cloned.1.call-start = ((), (), s32[]{:S(2)}) async-start(), calls=%async_computation.6 | async-start | bytes 1572864 | tf_op jit(solution)/shard_map/reduce_scatter | solution.py:145
  330.1 2.1 copy-start.2
  334.0 1.0 copy-start.3
  338.4 2.1 copy-start.2
  342.4 1.0 copy-start.3
  346.8 2.1 copy-start.2
  350.7 1.0 copy-start.3
  355.1 2.1 copy-start.2
  359.0 1.0 copy-start.3
  456.6 9.2 %copy-start.6 = (bf16[2048]{0:T(1024)(128)(2,1)S(1)}, bf16[2048]{0:T(1024)(128)(2,1)}, u32[]{:S(2)}) copy-start(bf16[2048]{0:T(1024)(128)(2,1)} %param.21) | copy-start | bytes 12292
  456.6 27.9 %copy-start.1 = (bf16[128,2048]{1,0:T(8,128)(2,1)S(1)}, bf16[128,2048]{1,0:T(8,128)(2,1)}, u32[]{:S(2)}) copy-start(bf16[128,2048]{1,0:T(8,128)(2,1)} %param.13) | copy-start | bytes 1572868
Sparse Core Ops, SparseCore 0:
  9.5 23.9 all-gather.8
  36.3 74.2 all-gather.10
  116.5 40.0 all-gather.18
  158.6 125.1 all-gather.14
  286.4 39.2 all-gather.12
  327.7 128.9 all-gather.16
  466.0 18.5 reduce-scatter.1
where the time goes:
time: 500 us
  waiting for transfers between devices  400 us (80%)
  matrix products  33.6 us (7%)
  other arithmetic  18.1 us (4%)
  local copies, waits for them, and re-layouts  16.7 us (3%)
  between operations  15 us (3%)
  blocking collectives  10.4 us (2%)
  loops' own time  5.46 us (1%)
    all_gather x1, waiting for transfers between devices, per_device(): lax.all_gather(w_query, 'seq', axis=0, tiled=True)  124 us
    all_gather x1, waiting for transfers between devices, per_device(): lax.all_gather(w_out, 'seq', axis=1, tiled=True)  94.8 us
    all_gather x1, waiting for transfers between devices, per_device(): lax.all_gather(key_value_weight, 'seq', axis=0, tiled=True)  75.6 us
    all_gather x1, waiting for transfers between devices, per_device(): value_piece = lax.all_gather(value_rows, 'seq', axis=0, tiled=True)  35.1 us
    all_gather x1, waiting for transfers between devices, per_device(): key_piece = lax.all_gather(rotated_keys, 'seq', axis=0, tiled=True)  32.3 us
    reduce_scatter x1, waiting for transfers between devices, per_device(): lax.psum_scatter(partial_out.astype(jnp.bfloat16), 'tp', scatter_dimensio...  18.7 us
    all_gather x1, waiting for transfers between devices, per_device(): lax.all_gather(hidden_in, 'tp', axis=1, tiled=True)  17.4 us
  transfers between devices with their start and end apart: 7, of which 7 were waited for; matrix products, arithmetic and copies ran while one was open for 9% of the time, Pallas kernels for 0%

commit v1 on v0

--- a/solution.py
+++ b/solution.py
@@ -61,12 +61,23 @@
         preferred_element_type=jnp.float32,
     )
     columns = normed_in
-    pair_proj = jnp.einsum(
-        "tr,rkc->tkc",
-        columns,
-        lax.all_gather(key_value_weight, "seq", axis=0, tiled=True),
-        preferred_element_type=jnp.float32,
-    )
+    a_next = jax.lax.axis_size("seq")
+    block_out = jax.lax.axis_index("seq")
+    piece_now, vec_out, res = (a_next, block_out, key_value_weight.shape[0])
+    xs_all = [(pp, (pp + 1) % piece_now) for pp in range(piece_now)]
+    lower, pair_proj = (key_value_weight, None)
+    for d in tuple(range(piece_now)):
+        all_values = jax.lax.ppermute(lower, "seq", xs_all) if d < piece_now - 1 else None
+        b_next = jnp.einsum(
+            "tr,rkc->tkc",
+            lax.dynamic_slice_in_dim(
+                columns, (vec_out - d) % piece_now * res, lower.shape[0], axis=1
+            ),
+            lower,
+            preferred_element_type=jnp.float32,
+        )
+        pair_proj = b_next if pair_proj is None else pair_proj + b_next
+        lower = all_values
     query_heads = w_query.shape[1] // HEAD_SIZE
     kv_heads = key_value_weight.shape[2] // HEAD_SIZE
     query_proj = query_proj + bias_query.astype(jnp.float32)[None, :]

time: 500 us -> 563 us (1.13)
  waiting for transfers between devices: 400 us -> 463 us
    ppermute x0 -> x15, waiting for transfers between devices: none -> 158 us  [per_device(): jax.lax.ppermute(lower, 'seq', xs_all)]
    all_gather x1 -> x0, waiting for transfers between devices: 75.6 us -> none  [per_device(): lax.all_gather(key_value_weight, 'seq', axis=0, tiled=True)]
    all_gather x1, waiting for transfers between devices: 17.4 us -> 0.01 us  [per_device(): lax.all_gather(hidden_in, 'tp', axis=1, tiled=True)]
  transfers between devices with their start and end apart: 7 -> 21, of which waited for: 7 -> 20; matrix products, arithmetic and copies ran while one was open for 9% -> 9% of each run, Pallas kernels for 0% -> 0%
where the time goes in v1:
time: 563 us
  waiting for transfers between devices  463 us (82%)
  matrix products  32.2 us (6%)
  other arithmetic  20 us (4%)
  local copies, waits for them, and re-layouts  16 us (3%)
  between operations  15.2 us (3%)
  blocking collectives  9.43 us (2%)
  loops' own time  5.71 us (1%)
    ppermute x15, waiting for transfers between devices, per_device(): jax.lax.ppermute(lower, 'seq', xs_all)  158 us
    all_gather x1, waiting for transfers between devices, per_device(): lax.all_gather(w_query, 'seq', axis=0, tiled=True)  124 us
    all_gather x1, waiting for transfers between devices, per_device(): lax.all_gather(w_out, 'seq', axis=1, tiled=True)  94.5 us
    all_gather x1, waiting for transfers between devices, per_device(): value_piece = lax.all_gather(value_rows, 'seq', axis=0, tiled=True)  34 us
    all_gather x1, waiting for transfers between devices, per_device(): key_piece = lax.all_gather(rotated_keys, 'seq', axis=0, tiled=True)  32.4 us
    reduce_scatter x1, waiting for transfers between devices, per_device(): lax.psum_scatter(partial_out.astype(jnp.bfloat16), 'tp', scatter_dimensio...  18.7 us
  transfers between devices with their start and end apart: 21, of which 20 were waited for; matrix products, arithmetic and copies ran while one was open for 9% of the time, Pallas kernels for 0%

profile of v1, /device:TPU:0, one launch (start us, length us, event | category | flops | bytes accessed | tf_op | source)
XLA Modules:
  0.0 562.6 jit_solution(17275331197739798459)
XLA Ops:
  7.2 1.1 copy.48
  8.9 11.8 %collective-permute-done = bf16[256,2,512]{2,0,1:T(8,128)(2,1)S(1)} collective-permute-done((bf16[256,2,512]{2,0,1:T(8,128)(2,1)S(1)}, bf16[256,2,512]{2,0,1:T(8,128)(2,1)S(1)}, u32[]{:S(2)}, u32[]{:S(2)}) %collective-permute-start) | collective-permute-done | bytes 524320 | tf_op jit(solution)/shard_map/ppermute | solution.py:70
  20.7 11.3 %collective-permute-done.1 = bf16[256,2,512]{2,0,1:T(8,128)(2,1)S(1)} collective-permute-done((bf16[256,2,512]{2,0,1:T(8,128)(2,1)S(1)}, bf16[256,2,512]{2,0,1:T(8,128)(2,1)S(1)}, u32[]{:S(2)}, u32[]{:S(2)}) %collective-permute-start.1) | collective-permute-done | bytes 524320 | tf_op jit(solution)/shard_map/ppermute | solution.py:70
  32.0 11.3 %collective-permute-done.2 = bf16[256,2,512]{2,0,1:T(8,128)(2,1)S(1)} collective-permute-done((bf16[256,2,512]{2,0,1:T(8,128)(2,1)S(1)}, bf16[256,2,512]{2,0,1:T(8,128)(2,1)S(1)}, u32[]{:S(2)}, u32[]{:S(2)}) %collective-permute-start.2) | collective-permute-done | bytes 524320 | tf_op jit(solution)/shard_map/ppermute | solution.py:70
  43.4 11.3 %collective-permute-done.3 = bf16[256,2,512]{2,0,1:T(8,128)(2,1)S(1)} collective-permute-done((bf16[256,2,512]{2,0,1:T(8,128)(2,1)S(1)}, bf16[256,2,512]{2,0,1:T(8,128)(2,1)S(1)}, u32[]{:S(2)}, u32[]{:S(2)}) %collective-permute-start.3) | collective-permute-done | bytes 524320 | tf_op jit(solution)/shard_map/ppermute | solution.py:70
  54.8 11.2 %collective-permute-done.4 = bf16[256,2,512]{2,0,1:T(8,128)(2,1)S(1)} collective-permute-done((bf16[256,2,512]{2,0,1:T(8,128)(2,1)S(1)}, bf16[256,2,512]{2,0,1:T(8,128)(2,1)S(1)}, u32[]{:S(2)}, u32[]{:S(2)}) %collective-permute-start.4) | collective-permute-done | bytes 524320 | tf_op jit(solution)/shard_map/ppermute | solution.py:70
  66.0 11.3 %collective-permute-done.5 = bf16[256,2,512]{2,0,1:T(8,128)(2,1)S(1)} collective-permute-done((bf16[256,2,512]{2,0,1:T(8,128)(2,1)S(1)}, bf16[256,2,512]{2,0,1:T(8,128)(2,1)S(1)}, u32[]{:S(2)}, u32[]{:S(2)}) %collective-permute-start.5) | collective-permute-done | bytes 524320 | tf_op jit(solution)/shard_map/ppermute | solution.py:70
  77.3 4.5 all-gather
  81.8 0.7 convert_element_type.69
  82.5 1.6 fusion.18
  84.2 4.4 collective-permute-done.6
  88.6 1.7 fusion.20
  90.6 9.3 %collective-permute-done.7 = bf16[256,2,512]{2,0,1:T(8,128)(2,1)S(1)} collective-permute-done((bf16[256,2,512]{2,0,1:T(8,128)(2,1)S(1)}, bf16[256,2,512]{2,0,1:T(8,128)(2,1)S(1)}, u32[]{:S(2)}, u32[]{:S(2)}) %collective-permute-start.7) | collective-permute-done | bytes 524320 | tf_op jit(solution)/shard_map/ppermute | solution.py:70
  100.4 10.8 %collective-permute-done.8 = bf16[256,2,512]{2,0,1:T(8,128)(2,1)S(1)} collective-permute-done((bf16[256,2,512]{2,0,1:T(8,128)(2,1)S(1)}, bf16[256,2,512]{2,0,1:T(8,128)(2,1)S(1)}, u32[]{:S(2)}, u32[]{:S(2)}) %collective-permute-start.8) | collective-permute-done | bytes 524320 | tf_op jit(solution)/shard_map/ppermute | solution.py:70
  111.7 10.8 %collective-permute-done.9 = bf16[256,2,512]{2,0,1:T(8,128)(2,1)S(1)} collective-permute-done((bf16[256,2,512]{2,0,1:T(8,128)(2,1)S(1)}, bf16[256,2,512]{2,0,1:T(8,128)(2,1)S(1)}, u32[]{:S(2)}, u32[]{:S(2)}) %collective-permute-start.9) | collective-permute-done | bytes 524320 | tf_op jit(solution)/shard_map/ppermute | solution.py:70
  123.0 10.8 %collective-permute-done.10 = bf16[256,2,512]{2,0,1:T(8,128)(2,1)S(1)} collective-permute-done((bf16[256,2,512]{2,0,1:T(8,128)(2,1)S(1)}, bf16[256,2,512]{2,0,1:T(8,128)(2,1)S(1)}, u32[]{:S(2)}, u32[]{:S(2)}) %collective-permute-start.10) | collective-permute-done | bytes 524320 | tf_op jit(solution)/shard_map/ppermute | solution.py:70
  134.3 10.8 %collective-permute-done.11 = bf16[256,2,512]{2,0,1:T(8,128)(2,1)S(1)} collective-permute-done((bf16[256,2,512]{2,0,1:T(8,128)(2,1)S(1)}, bf16[256,2,512]{2,0,1:T(8,128)(2,1)S(1)}, u32[]{:S(2)}, u32[]{:S(2)}) %collective-permute-start.11) | collective-permute-done | bytes 524320 | tf_op jit(solution)/shard_map/ppermute | solution.py:70
  145.6 10.8 %collective-permute-done.12 = bf16[256,2,512]{2,0,1:T(8,128)(2,1)S(1)} collective-permute-done((bf16[256,2,512]{2,0,1:T(8,128)(2,1)S(1)}, bf16[256,2,512]{2,0,1:T(8,128)(2,1)S(1)}, u32[]{:S(2)}, u32[]{:S(2)}) %collective-permute-start.12) | collective-permute-done | bytes 524320 | tf_op jit(solution)/shard_map/ppermute | solution.py:70
  156.9 10.8 %collective-permute-done.13 = bf16[256,2,512]{2,0,1:T(8,128)(2,1)S(1)} collective-permute-done((bf16[256,2,512]{2,0,1:T(8,128)(2,1)S(1)}, bf16[256,2,512]{2,0,1:T(8,128)(2,1)S(1)}, u32[]{:S(2)}, u32[]{:S(2)}) %collective-permute-start.13) | collective-permute-done | bytes 524320 | tf_op jit(solution)/shard_map/ppermute | solution.py:70
  168.2 10.8 %collective-permute-done.14 = bf16[256,2,512]{2,0,1:T(8,128)(2,1)S(1)} collective-permute-done((bf16[256,2,512]{2,0,1:T(8,128)(2,1)S(1)}, bf16[256,2,512]{2,0,1:T(8,128)(2,1)S(1)}, u32[]{:S(2)}, u32[]{:S(2)}) %collective-permute-start.14) | collective-permute-done | bytes 524320 | tf_op jit(solution)/shard_map/ppermute | solution.py:70
  179.3 0.7 slice.40
  180.0 0.7 all-gather.12.cloned.1.call-update
  183.0 0.8 copy.50
  184.7 0.7 iota_add_fusion.1
  185.4 34.0 %all-gather.16.cloned.1.call-done = bf16[2048,1,512]{2,0,1:T(8,128)(2,1)} async-done(((bf16[128,1,512]{2,0,1:T(8,128)(2,1)}), bf16[2048,1,512]{2,0,1:T(8,128)(2,1)}) %all-gather.16.cloned.1.call-update) | async-done | bytes 2097168 | tf_op jit(solution)/shard_map/all_gather | solution.py:107
  219.3 2.9 copy.53
  222.3 124.4 %all-gather.12.cloned.1.call-done = bf16[4096,2048]{1,0:T(8,128)(2,1)} async-done(((bf16[256,2048]{1,0:T(8,128)(2,1)}), bf16[4096,2048]{1,0:T(8,128)(2,1)}) %all-gather.12.cloned.1.call-update) | async-done | bytes 16777232 | tf_op jit(solution)/shard_map/all_gather | solution.py:60
  346.7 8.1 %fusion.21 = f32[16,8,16,128]{3,1,2,0:T(8,128)S(1)} fusion(bf16[128,4096]{1,0:T(8,128)(2,1)S(1)} %fusion.20, bf16[4096,2048]{1,0:T(8,128)(2,1)} %all-gather.12.cloned.1.call-done, f32[2048]{0:T(1024)S(1)} %convert_element_type.72), kind=kOutput, calls=%fused_computation.38 | convolution fusion | flops 2147745792 | bytes 18882560 | tf_op jit(solution)/shard_map/dot_general | solution.py:58
  356.1 32.4 %all-gather.10.cloned.1.call-done = bf16[2048,512]{0,1:T(8,128)(2,1)} async-done(((bf16[128,512]{0,1:T(8,128)(2,1)}), bf16[2048,512]{0,1:T(8,128)(2,1)}) %all-gather.10.cloned.1.call-update) | async-done | bytes 2097168 | tf_op jit(solution)/shard_map/all_gather | solution.py:106
  388.5 1.1 broadcast_in_dim.105
  389.6 33.5 %while.20 = (s32[]{:T(128)}, f32[4,512]{1,0:T(4,128)S(1)}, f32[4,512]{1,0:T(4,128)S(1)}, f32[4,512,128]{2,1,0:T(8,128)}, s32[16]{0:T(128)S(1)}, /*index=5*/s32[]...) while((s32[]{:T(128)}, f32[4,512]{1,0:T(4,128)S(1)}, ...), condition=%wide.region_10.11_spmd.clone, body=%wide.region_3.10_spmd.clone.sunk | while | flops 551332864 | bytes 27935680 | solution.py:144
  391.7 6.3 %conditional.3 = ((f32[4,512]{1,0:T(4,128)S(1)}, f32[4,512]{1,0:T(4,128)S(1)}, f32[4,512,128]{2,1,0:T(8,128)})) conditional(s32[]{:T(128)} %convert_element_type.109, (f32[4,512]{1,0:T(4,128)S(1)}, f32[4,512]{1,0:T(4,128)S(1)}, f32[4,512,128]{2,1,0:T(8,128)}) %tuple.77, (s32[512]{0:T(512)S(1)}, s32[128]{0:T(128)S(1)}, s32[]{:T(128)}, ...), branch_computations={%region_6.6_spmd, %region_7.9_spmd} | conditional | flops 551292928 | bytes 27925118 | solution.py:142
  391.9 1.1 constant_dynamic-slice_fusion
  393.1 1.0 fusion.2
  394.1 1.0 fusion.4
  395.2 1.8 fusion.8
  397.0 1.0 copy-done.2
  398.1 0.6 fusion.101
  400.0 6.3 %conditional.3 = ((f32[4,512]{1,0:T(4,128)S(1)}, f32[4,512]{1,0:T(4,128)S(1)}, f32[4,512,128]{2,1,0:T(8,128)})) conditional(s32[]{:T(128)} %convert_element_type.109, (f32[4,512]{1,0:T(4,128)S(1)}, f32[4,512]{1,0:T(4,128)S(1)}, f32[4,512,128]{2,1,0:T(8,128)}) %tuple.77, (s32[512]{0:T(512)S(1)}, s32[128]{0:T(128)S(1)}, s32[]{:T(128)}, ...), branch_computations={%region_6.6_spmd, %region_7.9_spmd} | conditional | flops 551292928 | bytes 27925118 | solution.py:142
  400.3 1.2 constant_dynamic-slice_fusion
  401.5 1.0 fusion.2
  402.5 1.0 fusion.4
  403.6 1.8 fusion.8
  405.4 1.0 copy-done.2
  408.4 6.3 %conditional.3 = ((f32[4,512]{1,0:T(4,128)S(1)}, f32[4,512]{1,0:T(4,128)S(1)}, f32[4,512,128]{2,1,0:T(8,128)})) conditional(s32[]{:T(128)} %convert_element_type.109, (f32[4,512]{1,0:T(4,128)S(1)}, f32[4,512]{1,0:T(4,128)S(1)}, f32[4,512,128]{2,1,0:T(8,128)}) %tuple.77, (s32[512]{0:T(512)S(1)}, s32[128]{0:T(128)S(1)}, s32[]{:T(128)}, ...), branch_computations={%region_6.6_spmd, %region_7.9_spmd} | conditional | flops 551292928 | bytes 27925118 | solution.py:142
  408.7 1.1 constant_dynamic-slice_fusion
  409.8 1.0 fusion.2
  410.9 1.0 fusion.4
  412.0 1.8 fusion.8
  413.8 1.0 copy-done.2
  414.8 0.6 fusion.101
  416.8 6.3 %conditional.3 = ((f32[4,512]{1,0:T(4,128)S(1)}, f32[4,512]{1,0:T(4,128)S(1)}, f32[4,512,128]{2,1,0:T(8,128)})) conditional(s32[]{:T(128)} %convert_element_type.109, (f32[4,512]{1,0:T(4,128)S(1)}, f32[4,512]{1,0:T(4,128)S(1)}, f32[4,512,128]{2,1,0:T(8,128)}) %tuple.77, (s32[512]{0:T(512)S(1)}, s32[128]{0:T(128)S(1)}, s32[]{:T(128)}, ...), branch_computations={%region_6.6_spmd, %region_7.9_spmd} | conditional | flops 551292928 | bytes 27925118 | solution.py:142
  417.1 1.1 constant_dynamic-slice_fusion
  418.2 1.0 fusion.2
  419.3 1.0 fusion.4
  420.3 1.8 fusion.8
  422.1 1.0 copy-done.2
  423.1 1.6 divide_convert_fusion
  425.0 94.5 %all-gather.14.cloned.1.call-done = bf16[2048,4096]{1,0:T(8,128)(2,1)} async-done(((bf16[2048,256]{1,0:T(8,128)(2,1)}), bf16[2048,4096]{1,0:T(8,128)(2,1)}) %all-gather.14.cloned.1.call-update) | async-done | bytes 16777232 | tf_op jit(solution)/shard_map/all_gather | solution.py:153
  519.5 9.2 %convolution_convert_fusion = bf16[128,4096]{1,0:T(8,128)(2,1)} fusion(bf16[128,2048]{0,1:T(8,128)(2,1)S(1)} %bitcast.107, bf16[2048,4096]{1,0:T(8,128)(2,1)} %all-gather.14.cloned.1.call-done), kind=kOutput, calls=%fused_computation.31 | convolution fusion | flops 2148007936 | bytes 18350080 | tf_op jit(solution)/shard_map/dot_general | solution.py:151
  528.8 18.7 %reduce-scatter.2.cloned.1.call-done = bf16[128,2048]{1,0:T(8,128)(2,1)} async-done(((bf16[128,4096]{1,0:T(8,128)(2,1)}), bf16[128,2048]{1,0:T(8,128)(2,1)}) %reduce-scatter.2.cloned.1.call-update) | async-done | bytes 524304 | tf_op jit(solution)/shard_map/reduce_scatter | solution.py:156
  547.5 1.3 multiply_reduce_fusion
  548.8 4.9 psum.7
  553.7 2.0 multiply_convert_fusion
  (140 shorter events, 11.3 us)
Async XLA Ops:
  7.2 83.2 %copy-start.3 = (bf16[256,2,512]{2,1,0:T(2,128)(2,1)S(1)}, bf16[256,2,512]{2,1,0:T(2,128)(2,1)}, u32[]{:S(2)}) copy-start(bf16[256,2,512]{2,1,0:T(2,128)(2,1)} %param.18) | copy-start | bytes 1572868
  7.2 75.3 %all-gather.8.cloned.1.call-start = ((), (), s32[]{:S(2)}) async-start(), calls=%async_computation.1 | async-start | bytes 1572864 | tf_op jit(solution)/shard_map/all_gather | solution.py:49
  8.4 12.4 %collective-permute-start = (bf16[256,2,512]{2,0,1:T(8,128)(2,1)S(1)}, bf16[256,2,512]{2,0,1:T(8,128)(2,1)S(1)}, u32[]{:S(2)}, u32[]{:S(2)}) collective-permute-start(bf16[256,2,512]{2,0,1:T(8,128)(2,1)S(1)} %copy.48), channel_id=1, source_target_pairs={{0,2},{2,4},{4,6},{6,8},{8,10},{10,12},{12,14},{14,16},{16,18},{18... | collective-permute-start | bytes 1572872 | tf_op jit(solution)/shard_map/ppermute | solution.py:70
  20.7 22.6 %copy-start.4 = (bf16[256,2,512]{2,0,1:T(8,128)(2,1)}, bf16[256,2,512]{2,0,1:T(8,128)(2,1)S(1)}, u32[]{:S(2)}) copy-start(bf16[256,2,512]{2,0,1:T(8,128)(2,1)S(1)} %collective-permute-done) | copy-start | bytes 1572868
  20.7 11.3 %collective-permute-start.1 = (bf16[256,2,512]{2,0,1:T(8,128)(2,1)S(1)}, bf16[256,2,512]{2,0,1:T(8,128)(2,1)S(1)}, u32[]{:S(2)}, u32[]{:S(2)}) collective-permute-start(bf16[256,2,512]{2,0,1:T(8,128)(2,1)S(1)} %collective-permute-done), channel_id=1, source_target_pairs={{0,2},{2,4},{4,6},{6,8},{8,10},{10,12},{12,14},{14,16},{16,18},{18... | collective-permute-start | bytes 1572872 | tf_op jit(solution)/shard_map/ppermute | solution.py:70
  32.0 22.6 %copy-start.10 = (bf16[256,2,512]{2,0,1:T(8,128)(2,1)}, bf16[256,2,512]{2,0,1:T(8,128)(2,1)S(1)}, u32[]{:S(2)}) copy-start(bf16[256,2,512]{2,0,1:T(8,128)(2,1)S(1)} %collective-permute-done.1) | copy-start | bytes 1572868
  32.0 11.3 %collective-permute-start.2 = (bf16[256,2,512]{2,0,1:T(8,128)(2,1)S(1)}, bf16[256,2,512]{2,0,1:T(8,128)(2,1)S(1)}, u32[]{:S(2)}, u32[]{:S(2)}) collective-permute-start(bf16[256,2,512]{2,0,1:T(8,128)(2,1)S(1)} %collective-permute-done.1), channel_id=1, source_target_pairs={{0,2},{2,4},{4,6},{6,8},{8,10},{10,12},{12,14},{14,16},{16,18},{18... | collective-permute-start | bytes 1572872 | tf_op jit(solution)/shard_map/ppermute | solution.py:70
  43.3 11.3 %copy-start.6 = (bf16[256,2,512]{2,0,1:T(8,128)(2,1)}, bf16[256,2,512]{2,0,1:T(8,128)(2,1)S(1)}, u32[]{:S(2)}) copy-start(bf16[256,2,512]{2,0,1:T(8,128)(2,1)S(1)} %collective-permute-done.2) | copy-start | bytes 1572868
  43.3 11.3 %collective-permute-start.3 = (bf16[256,2,512]{2,0,1:T(8,128)(2,1)S(1)}, bf16[256,2,512]{2,0,1:T(8,128)(2,1)S(1)}, u32[]{:S(2)}, u32[]{:S(2)}) collective-permute-start(bf16[256,2,512]{2,0,1:T(8,128)(2,1)S(1)} %collective-permute-done.2), channel_id=1, source_target_pairs={{0,2},{2,4},{4,6},{6,8},{8,10},{10,12},{12,14},{14,16},{16,18},{18... | collective-permute-start | bytes 1572872 | tf_op jit(solution)/shard_map/ppermute | solution.py:70
  54.7 34.0 %copy-start.8 = (bf16[256,2,512]{2,0,1:T(8,128)(2,1)}, bf16[256,2,512]{2,0,1:T(8,128)(2,1)S(1)}, u32[]{:S(2)}) copy-start(bf16[256,2,512]{2,0,1:T(8,128)(2,1)S(1)} %collective-permute-done.3) | copy-start | bytes 1572868
  54.7 11.4 %collective-permute-start.4 = (bf16[256,2,512]{2,0,1:T(8,128)(2,1)S(1)}, bf16[256,2,512]{2,0,1:T(8,128)(2,1)S(1)}, u32[]{:S(2)}, u32[]{:S(2)}) collective-permute-start(bf16[256,2,512]{2,0,1:T(8,128)(2,1)S(1)} %collective-permute-done.3), channel_id=1, source_target_pairs={{0,2},{2,4},{4,6},{6,8},{8,10},{10,12},{12,14},{14,16},{16,18},{18... | collective-permute-start | bytes 1572872 | tf_op jit(solution)/shard_map/ppermute | solution.py:70
  54.7 164.6 %all-gather.16.cloned.1.call-start = ((), (), s32[]{:S(2)}) async-start(), calls=%async_computation.6 | async-start | bytes 2228224 | tf_op jit(solution)/shard_map/all_gather | solution.py:107
  66.0 11.3 %collective-permute-start.5 = (bf16[256,2,512]{2,0,1:T(8,128)(2,1)S(1)}, bf16[256,2,512]{2,0,1:T(8,128)(2,1)S(1)}, u32[]{:S(2)}, u32[]{:S(2)}) collective-permute-start(bf16[256,2,512]{2,0,1:T(8,128)(2,1)S(1)} %collective-permute-done.4), channel_id=1, source_target_pairs={{0,2},{2,4},{4,6},{6,8},{8,10},{10,12},{12,14},{14,16},{16,18},{18... | collective-permute-start | bytes 1572872 | tf_op jit(solution)/shard_map/ppermute | solution.py:70
  77.3 11.3 %copy-start.14 = (bf16[256,2,512]{2,0,1:T(8,128)(2,1)}, bf16[256,2,512]{2,0,1:T(8,128)(2,1)S(1)}, u32[]{:S(2)}) copy-start(bf16[256,2,512]{2,0,1:T(8,128)(2,1)S(1)} %collective-permute-done.5) | copy-start | bytes 1572868
  77.3 11.3 %collective-permute-start.6 = (bf16[256,2,512]{2,0,1:T(8,128)(2,1)S(1)}, bf16[256,2,512]{2,0,1:T(8,128)(2,1)S(1)}, u32[]{:S(2)}, u32[]{:S(2)}) collective-permute-start(bf16[256,2,512]{2,0,1:T(8,128)(2,1)S(1)} %collective-permute-done.5), channel_id=1, source_target_pairs={{0,2},{2,4},{4,6},{6,8},{8,10},{10,12},{12,14},{14,16},{16,18},{18... | collective-permute-start | bytes 1572872 | tf_op jit(solution)/shard_map/ppermute | solution.py:70
  82.5 17.4 %copy-start.5 = (bf16[256,2,512]{2,0,1:T(8,128)(2,1)S(1)}, bf16[256,2,512]{2,0,1:T(8,128)(2,1)}, u32[]{:S(2)}) copy-start(bf16[256,2,512]{2,0,1:T(8,128)(2,1)} %copy-done.4) | copy-start | bytes 1572868
  82.5 17.7 %copy-start.11 = (bf16[256,2,512]{2,0,1:T(8,128)(2,1)S(1)}, bf16[256,2,512]{2,0,1:T(8,128)(2,1)}, u32[]{:S(2)}) copy-start(bf16[256,2,512]{2,0,1:T(8,128)(2,1)} %copy-done.10) | copy-start | bytes 1572868
  82.5 28.7 %copy-start.7 = (bf16[256,2,512]{2,0,1:T(8,128)(2,1)S(1)}, bf16[256,2,512]{2,0,1:T(8,128)(2,1)}, u32[]{:S(2)}) copy-start(bf16[256,2,512]{2,0,1:T(8,128)(2,1)} %copy-done.6) | copy-start | bytes 1572868
  88.6 11.3 %copy-start.12 = (bf16[256,2,512]{2,0,1:T(8,128)(2,1)}, bf16[256,2,512]{2,0,1:T(8,128)(2,1)S(1)}, u32[]{:S(2)}) copy-start(bf16[256,2,512]{2,0,1:T(8,128)(2,1)S(1)} %collective-permute-done.6) | copy-start | bytes 1572868
  88.6 11.3 %collective-permute-start.7 = (bf16[256,2,512]{2,0,1:T(8,128)(2,1)S(1)}, bf16[256,2,512]{2,0,1:T(8,128)(2,1)S(1)}, u32[]{:S(2)}, u32[]{:S(2)}) collective-permute-start(bf16[256,2,512]{2,0,1:T(8,128)(2,1)S(1)} %collective-permute-done.6), channel_id=1, source_target_pairs={{0,2},{2,4},{4,6},{6,8},{8,10},{10,12},{12,14},{14,16},{16,18},{18... | collective-permute-start | bytes 1572872 | tf_op jit(solution)/shard_map/ppermute | solution.py:70
  90.4 21.1 %copy-start.9 = (bf16[256,2,512]{2,0,1:T(8,128)(2,1)S(1)}, bf16[256,2,512]{2,0,1:T(8,128)(2,1)}, u32[]{:S(2)}) copy-start(bf16[256,2,512]{2,0,1:T(8,128)(2,1)} %copy-done.8) | copy-start | bytes 1572868
  90.6 32.1 %copy-start.15 = (bf16[256,2,512]{2,0,1:T(8,128)(2,1)S(1)}, bf16[256,2,512]{2,0,1:T(8,128)(2,1)}, u32[]{:S(2)}) copy-start(bf16[256,2,512]{2,0,1:T(8,128)(2,1)} %copy-done.14) | copy-start | bytes 1572868
  99.9 11.3 %collective-permute-start.8 = (bf16[256,2,512]{2,0,1:T(8,128)(2,1)S(1)}, bf16[256,2,512]{2,0,1:T(8,128)(2,1)S(1)}, u32[]{:S(2)}, u32[]{:S(2)}) collective-permute-start(bf16[256,2,512]{2,0,1:T(8,128)(2,1)S(1)} %collective-permute-done.7), channel_id=1, source_target_pairs={{0,2},{2,4},{4,6},{6,8},{8,10},{10,12},{12,14},{14,16},{16,18},{18... | collective-permute-start | bytes 1572872 | tf_op jit(solution)/shard_map/ppermute | solution.py:70
  100.2 33.7 %copy-start.13 = (bf16[256,2,512]{2,0,1:T(8,128)(2,1)S(1)}, bf16[256,2,512]{2,0,1:T(8,128)(2,1)}, u32[]{:S(2)}) copy-start(bf16[256,2,512]{2,0,1:T(8,128)(2,1)} %copy-done.12) | copy-start | bytes 1572868
  111.2 11.3 %collective-permute-start.9 = (bf16[256,2,512]{2,0,1:T(8,128)(2,1)S(1)}, bf16[256,2,512]{2,0,1:T(8,128)(2,1)S(1)}, u32[]{:S(2)}, u32[]{:S(2)}) collective-permute-start(bf16[256,2,512]{2,0,1:T(8,128)(2,1)S(1)} %collective-permute-done.8), channel_id=1, source_target_pairs={{0,2},{2,4},{4,6},{6,8},{8,10},{10,12},{12,14},{14,16},{16,18},{18... | collective-permute-start | bytes 1572872 | tf_op jit(solution)/shard_map/ppermute | solution.py:70
  122.5 11.3 %collective-permute-start.10 = (bf16[256,2,512]{2,0,1:T(8,128)(2,1)S(1)}, bf16[256,2,512]{2,0,1:T(8,128)(2,1)S(1)}, u32[]{:S(2)}, u32[]{:S(2)}) collective-permute-start(bf16[256,2,512]{2,0,1:T(8,128)(2,1)S(1)} %collective-permute-done.9), channel_id=1, source_target_pairs={{0,2},{2,4},{4,6},{6,8},{8,10},{10,12},{12,14},{14,16},{16,18},{18... | collective-permute-start | bytes 1572872 | tf_op jit(solution)/shard_map/ppermute | solution.py:70
  133.8 11.3 %collective-permute-start.11 = (bf16[256,2,512]{2,0,1:T(8,128)(2,1)S(1)}, bf16[256,2,512]{2,0,1:T(8,128)(2,1)S(1)}, u32[]{:S(2)}, u32[]{:S(2)}) collective-permute-start(bf16[256,2,512]{2,0,1:T(8,128)(2,1)S(1)} %collective-permute-done.10), channel_id=1, source_target_pairs={{0,2},{2,4},{4,6},{6,8},{8,10},{10,12},{12,14},{14,16},{16,18},{18... | collective-permute-start | bytes 1572872 | tf_op jit(solution)/shard_map/ppermute | solution.py:70
  145.1 11.3 %collective-permute-start.12 = (bf16[256,2,512]{2,0,1:T(8,128)(2,1)S(1)}, bf16[256,2,512]{2,0,1:T(8,128)(2,1)S(1)}, u32[]{:S(2)}, u32[]{:S(2)}) collective-permute-start(bf16[256,2,512]{2,0,1:T(8,128)(2,1)S(1)} %collective-permute-done.11), channel_id=1, source_target_pairs={{0,2},{2,4},{4,6},{6,8},{8,10},{10,12},{12,14},{14,16},{16,18},{18... | collective-permute-start | bytes 1572872 | tf_op jit(solution)/shard_map/ppermute | solution.py:70
  156.4 11.3 %collective-permute-start.13 = (bf16[256,2,512]{2,0,1:T(8,128)(2,1)S(1)}, bf16[256,2,512]{2,0,1:T(8,128)(2,1)S(1)}, u32[]{:S(2)}, u32[]{:S(2)}) collective-permute-start(bf16[256,2,512]{2,0,1:T(8,128)(2,1)S(1)} %collective-permute-done.12), channel_id=1, source_target_pairs={{0,2},{2,4},{4,6},{6,8},{8,10},{10,12},{12,14},{14,16},{16,18},{18... | collective-permute-start | bytes 1572872 | tf_op jit(solution)/shard_map/ppermute | solution.py:70
  156.7 24.1 %copy-start.16 = (s32[16]{0:T(128)S(1)}, s32[16]{0:T(128)}, u32[]{:S(2)}) copy-start(s32[16]{0:T(128)} %param.14) | copy-start | bytes 196
  167.7 11.3 %collective-permute-start.14 = (bf16[256,2,512]{2,0,1:T(8,128)(2,1)S(1)}, bf16[256,2,512]{2,0,1:T(8,128)(2,1)S(1)}, u32[]{:S(2)}, u32[]{:S(2)}) collective-permute-start(bf16[256,2,512]{2,0,1:T(8,128)(2,1)S(1)} %collective-permute-done.13), channel_id=1, source_target_pairs={{0,2},{2,4},{4,6},{6,8},{8,10},{10,12},{12,14},{14,16},{16,18},{18... | collective-permute-start | bytes 1572872 | tf_op jit(solution)/shard_map/ppermute | solution.py:70
  168.0 16.7 %copy-start.17 = (bf16[2048]{0:T(1024)(128)(2,1)S(1)}, bf16[2048]{0:T(1024)(128)(2,1)}, u32[]{:S(2)}) copy-start(bf16[2048]{0:T(1024)(128)(2,1)} %param.17) | copy-start | bytes 12292
  180.0 166.7 %all-gather.12.cloned.1.call-start = ((), (), s32[]{:S(2)}) async-start(), calls=%async_computation.3 | async-start | bytes 17825792 | tf_op jit(solution)/shard_map/all_gather | solution.py:60
  180.7 207.8 %all-gather.10.cloned.1.call-start = ((), (), s32[]{:S(2)}) async-start(), calls=%async_computation.2 | async-start | bytes 2228224 | tf_op jit(solution)/shard_map/all_gather | solution.py:106
  183.8 335.7 %all-gather.14.cloned.1.call-start = ((), (), s32[]{:S(2)}) async-start(), calls=%async_computation.4 | async-start | bytes 17825792 | tf_op jit(solution)/shard_map/all_gather | solution.py:153
  184.4 363.1 %reduce-scatter.2.cloned.1.call-start = ((), (), s32[]{:S(2)}) async-start(), calls=%async_computation.5 | async-start | bytes 1572864 | tf_op jit(solution)/shard_map/reduce_scatter | solution.py:156
  393.1 2.1 copy-start.1
  397.0 1.0 copy-start.2
  401.5 2.1 copy-start.1
  405.4 1.0 copy-start.2
  409.8 2.1 copy-start.1
  413.8 1.0 copy-start.2
  418.2 2.1 copy-start.1
  422.1 1.0 copy-start.2
  519.5 9.2 %copy-start.18 = (bf16[2048]{0:T(1024)(128)(2,1)S(1)}, bf16[2048]{0:T(1024)(128)(2,1)}, u32[]{:S(2)}) copy-start(bf16[2048]{0:T(1024)(128)(2,1)} %param.21) | copy-start | bytes 12292
  519.5 27.9 %copy-start = (bf16[128,2048]{1,0:T(8,128)(2,1)S(1)}, bf16[128,2048]{1,0:T(8,128)(2,1)}, u32[]{:S(2)}) copy-start(bf16[128,2048]{1,0:T(8,128)(2,1)} %param.13) | copy-start | bytes 1572868
Sparse Core Ops, SparseCore 0:
  54.9 22.9 all-gather.7
  180.1 39.1 all-gather.15
  221.5 125.1 all-gather.11
  349.3 39.2 all-gather.9
  390.5 128.9 all-gather.13
  528.9 18.5 reduce-scatter.1
